TPU v7x, 32 devices: a whole 2x2x4 slice. The times are simulated.
32 devices in a mesh: pb: 4 (over x, core), dev: 8 (over z, y).
Axes of the slice: x: 2, y: 2, z: 4, core: 2. Of those that a mesh axis runs over, the one named last changes fastest.
Arguments:
- queries: bfloat16 [64, 768], P(('pb', 'dev')), may hold values from -6 to 6
- probes: int32 [64, 16], P(('pb', 'dev')), may hold values from 0 to 1023, all different within a row
- vectors: bfloat16 [16384, 768], P(('pb', 'dev')), may hold values from -0.4375 to 0.4375
- list_ids: int32 [16384], P(('pb', 'dev')), may hold values from 0 to 1023, as said below
Outputs:
- leaders: float32 [64, 100], P(('pb', 'dev'))
Inputs may be any that keep to these rules, and one draw needn't show every extreme that they name: `list_ids`: each list id names exactly 16 database vectors. `probes`: each query names 16 different lists.
All inputs are finite; a program needn't handle non-finite values.
Results may differ from a plain program's by a relative error of at most 0.0004.
Values may be sent and summed in bfloat16 or wider, within the bound.
A program may use at most 64 MiB of HBM per device.

v0:
```python
import math
import jax
import jax.numpy as jnp
from jax import lax
from jax.sharding import PartitionSpec as P

K = 100
NLIST = 1024
masked_value = -1e30


def filtered_scores(block_rows, block_probes, slab_part, list_onehot):
    products = lax.dot_general(
        block_rows, slab_part, (((1,), (1,)), ((), ())), preferred_element_type=jnp.float32
    )
    count = block_rows.shape[0]
    row_index = lax.broadcasted_iota(jnp.int32, block_probes.shape, 0)
    hits = (
        jnp.zeros((count, list_onehot.shape[0]), jnp.bfloat16)
        .at[row_index, block_probes]
        .set(jnp.bfloat16(1.0))
    )
    matches = jnp.dot(hits, list_onehot, preferred_element_type=jnp.float32)
    return jnp.where(matches > 0.5, products, jnp.float32(masked_value))


def local(queries, probes, vectors, list_ids):
    local_count = min(K, vectors.shape[0])
    list_index = lax.broadcasted_iota(jnp.int32, (NLIST, list_ids.shape[0]), 0)
    list_onehot = (list_index == list_ids[None, :]).astype(jnp.bfloat16)
    block_rows, block_probes = lax.all_gather((queries, probes), ("pb", "dev"), axis=0, tiled=True)
    count = block_rows.shape[0]
    width = math.gcd(count, 256)

    def one_block(block_args):
        rows_here, probes_here = block_args
        kept, _ = lax.top_k(
            filtered_scores(rows_here, probes_here, vectors, list_onehot), local_count
        )
        return kept

    kept = lax.map(
        one_block,
        (
            block_rows.reshape(count // width, width, block_rows.shape[1]),
            block_probes.reshape(count // width, width, block_probes.shape[1]),
        ),
    )
    candidates = kept.reshape(count, local_count)
    pooled = lax.all_to_all(
        lax.all_to_all(candidates, "pb", split_axis=0, concat_axis=1, tiled=True),
        "dev",
        split_axis=0,
        concat_axis=1,
        tiled=True,
    )
    leaders, _ = lax.top_k(pooled, K)
    return leaders


def solution(mesh):
    return jax.shard_map(
        local,
        mesh=mesh,
        in_specs=(
            P(("pb", "dev"), None),
            P(("pb", "dev"), None),
            P(("pb", "dev"), None),
            P(("pb", "dev")),
        ),
        out_specs=P(("pb", "dev"), None),
        check_vma=False,
    )
```

profile of v0, /device:TPU:0, one launch (start us, length us, event | category | flops | bytes accessed | tf_op | source)
XLA Modules:
  0.0 173.4 jit_solution(18283265919945762596)
XLA Ops:
  0.0 0.0 copy-start
  0.0 0.0 copy-start.1
  0.0 70.2 %all-gather = s32[32,2,16]{2,1,0:T(2,128)S(1)} all-gather(s32[1,2,16]{2,1,0:T(2,128)} %bitcast.16), channel_id=1, replica_groups=mesh['pb'=4,'dev'=8] {'pb','dev'}, dimensions={0}, use_global_device_ids=true | all-gather | bytes 4224 | tf_op jit(solution)/shard_map/all_gather | solution.py:31
  70.2 0.1 copy.13
  70.3 0.7 multiply_reduce_fusion
  71.0 0.7 and_reduce_fusion
  71.8 0.1 copy.16
  71.9 0.1 reshape.32
  71.9 7.7 %scatter_custom_fusion = bf16[65536]{0:T(1024)(128)(2,1)S(1)} fusion(s32[1024]{0:T(1024)S(1)} %reshape.32, bf16[1024]{0:T(1024)(128)(2,1)S(1)} %broadcast.64, bf16[]{:T(256)} %constant.41.clone.1), kind=kCustom, calls=%fused_computation.6 | custom fusion | bytes 131074
  79.6 0.1 reshape.31
  79.7 64.1 %all-gather.1 = bf16[32,2,768]{2,1,0:T(2,128)(2,1)S(1)} all-gather(bf16[1,2,768]{2,1,0:T(2,128)(2,1)} %bitcast.15), channel_id=1, replica_groups=mesh['pb'=4,'dev'=8] {'pb','dev'}, dimensions={0}, use_global_device_ids=true | all-gather | bytes 101376 | tf_op jit(solution)/shard_map/all_gather | solution.py:31
  143.8 0.0 copy-done.1
  143.8 0.5 fusion.1
  144.3 0.0 copy-done
  144.3 0.4 convolution_select_fusion
  144.7 3.2 %sort_prefixfusion = f32[64,100]{1,0:T(8,128)S(1)} fusion(f32[64,512]{1,0:T(8,128)S(1)} %convolution_select_fusion), kind=kCustom, calls=%top_k.14.sort_prefix | custom fusion | flops 491520 | bytes 156672 | tf_op jit(solution)/shard_map/while/body/eval_jaxpr/top_k | solution.py:37
  147.9 6.3 %all_to_all.35 = f32[4,16,100]{2,1,0:T(8,128)S(1)} all-to-all(f32[4,16,100]{2,1,0:T(8,128)S(1)} %bitcast.11), channel_id=1, replica_groups=mesh['pb'=4,'dev'=8] {'pb'}, dimensions={0} | all-to-all | bytes 51200 | tf_op jit(solution)/shard_map/all_to_all | solution.py:51
  154.2 0.1 all_to_all.29
  154.3 10.0 %all_to_all.36 = f32[8,2,400]{2,1,0:T(2,128)S(1)} all-to-all(f32[8,2,400]{2,1,0:T(2,128)S(1)} %all_to_all.29), channel_id=1, replica_groups=mesh['pb'=4,'dev'=8] {'dev'}, dimensions={0} | all-to-all | bytes 51200 | tf_op jit(solution)/shard_map/all_to_all | solution.py:50
  164.3 0.1 all_to_all.32
  164.4 8.4 %top_k.20 = (f32[2,3200]{1,0:T(2,128)S(1)}, s32[2,3200]{1,0:T(2,128)}) sort(f32[2,3200]{1,0:T(2,128)S(1)} %all_to_all.32, s32[2,3200]{1,0:T(2,128)S(1)} %iota.24), dimensions={1}, to_apply=%region_2.3 | sort | flops 83200 | bytes 102400 | tf_op jit(solution)/shard_map/top_k | solution.py:57
  172.8 0.6 top_k.21
  (8 shorter events, 0.1 us)
Async XLA Ops:
  0.0 144.3 %copy-start = (bf16[512,768]{1,0:T(8,128)(2,1)S(1)}, bf16[512,768]{1,0:T(8,128)(2,1)}, u32[]{:S(2)}) copy-start(bf16[512,768]{1,0:T(8,128)(2,1)} %param.6) | copy-start | bytes 2359300
  0.0 143.8 %copy-start.1 = (s32[512]{0:T(512)S(1)}, s32[512]{0:T(512)}, u32[]{:S(2)}) copy-start(s32[512]{0:T(512)} %param.7) | copy-start | bytes 6148
where the time goes:
time: 174 us; the launch traced here: 173 us
  blocking collectives  151 us (87%)
  other arithmetic  13.1 us (8%)
  local copies, waits for them, and re-layouts  8.8 us (5%)
    all_gather x2, blocking collectives, local(): lax.all_gather((queries, probes), ('pb', 'dev'), axis=0, tiled=True)  134 us
    all_to_all x1, blocking collectives, local(): lax.all_to_all(lax.all_to_all(candidates, 'pb', split_axis=0, concat_axis...  9.97 us
    top_k x1, other arithmetic, local(): leaders, _ = lax.top_k(pooled, K)  8.39 us
    unnamed x10, local copies, waits for them, and re-layouts  7.93 us
    all_to_all x1, blocking collectives, local(): lax.all_to_all(candidates, 'pb', split_axis=0, concat_axis=1, tiled=True)  6.3 us

commit v1 on v0

--- a/solution.py
+++ b/solution.py
@@ -7,6 +7,34 @@
 K = 100
 NLIST = 1024
 masked_value = -1e30
+
+
+def racks_mark(xx, array_axis, field_in):
+    f_next = xx.shape
+    everything = xx.reshape(
+        *f_next[:array_axis], field_in, f_next[array_axis] // field_in, *f_next[array_axis + 1 :]
+    )
+    row_out = jnp.moveaxis(everything, array_axis, 0)
+    return row_out
+
+
+def clusters_mark(inner_x, out_dim):
+    inner_x = jnp.moveaxis(inner_x, 0, out_dim)
+    r1 = inner_x.shape
+    g_now = inner_x.reshape(*r1[:out_dim], r1[out_dim] * r1[out_dim + 1], *r1[out_dim + 2 :])
+    return g_now
+
+
+def use_the_point(t0, chip_axis, u, body):
+    top, outer = (lax.axis_size(chip_axis), lax.axis_index(chip_axis))
+    carry = racks_mark(t0, u, top)
+    grid = [carry[outer]]
+    for dd in [*range(1, top)]:
+        far_arr = carry[outer ^ dd]
+        grid.append(lax.ppermute(far_arr, chip_axis, perm=[(i0, i0 ^ dd) for i0 in range(top)]))
+    carry = jnp.stack(grid)[outer ^ jnp.arange(top)]
+    block_now = clusters_mark(carry, body)
+    return block_now
 
 
 def filtered_scores(block_rows, block_probes, slab_part, list_onehot):
@@ -47,12 +75,8 @@
         ),
     )
     candidates = kept.reshape(count, local_count)
-    pooled = lax.all_to_all(
-        lax.all_to_all(candidates, "pb", split_axis=0, concat_axis=1, tiled=True),
-        "dev",
-        split_axis=0,
-        concat_axis=1,
-        tiled=True,
+    pooled = use_the_point(
+        lax.all_to_all(candidates, "pb", split_axis=0, concat_axis=1, tiled=True), "dev", 0, 1
     )
     leaders, _ = lax.top_k(pooled, K)
     return leaders

time: 174 us -> 180 us (1.034)
  blocking collectives: 151 us -> 134 us
  starting transfers between devices: 0 us -> 14.9 us
  waiting for transfers between devices: 0 us -> 6.65 us
    all_to_all x2 -> x0, blocking collectives: 16.3 us -> none  [the longest x1 9.97 us: local(): lax.all_to_all(lax.all_to_all(candidates, 'pb', split_axis=0, concat_axis...]
    ppermute x0 -> x7, starting transfers between devices: none -> 11.5 us  [use_the_point(): lax.ppermute(far_arr, chip_axis, perm=[(i0, i0 ^ dd) for i0 in range(top)])]
    all_to_all x0 -> x1, waiting for transfers between devices: none -> 3.67 us  [local(): lax.all_to_all(candidates, 'pb', split_axis=0, concat_axis=1, tiled=True)]
    all_to_all x0 -> x1, starting transfers between devices: none -> 3.44 us  [local(): lax.all_to_all(candidates, 'pb', split_axis=0, concat_axis=1, tiled=True)]
    ppermute x0 -> x7, waiting for transfers between devices: none -> 2.98 us  [use_the_point(): lax.ppermute(far_arr, chip_axis, perm=[(i0, i0 ^ dd) for i0 in range(top)])]
    unnamed x10 -> x16, local copies, waits for them, and re-layouts: 7.93 us -> 7.98 us
  transfers between devices with their start and end apart: 0 -> 8, of which waited for: 0 -> 3; matrix products, arithmetic and copies ran while one was open for 0% -> 0% of each run, Pallas kernels for 0% -> 0%
where the time goes in v1:
time: 180 us
  blocking collectives  134 us (74%)
  starting transfers between devices  14.9 us (8%)
  other arithmetic  13.7 us (8%)
  local copies, waits for them, and re-layouts  9.47 us (5%)
  waiting for transfers between devices  6.65 us (4%)
    all_gather x2, blocking collectives, local(): lax.all_gather((queries, probes), ('pb', 'dev'), axis=0, tiled=True)  134 us
    ppermute x7, starting transfers between devices, use_the_point(): lax.ppermute(far_arr, chip_axis, perm=[(i0, i0 ^ dd) for i0 in range(top)])  11.5 us
    top_k x1, other arithmetic, local(): leaders, _ = lax.top_k(pooled, K)  8.39 us
    unnamed x16, local copies, waits for them, and re-layouts  7.98 us
    top_k x1, other arithmetic, one_block(): lax.top_k(filtered_scores(rows_here, probes_here, vectors, list_onehot),...  3.79 us
    all_to_all x1, waiting for transfers between devices, local(): lax.all_to_all(candidates, 'pb', split_axis=0, concat_axis=1, tiled=True)  3.67 us
  transfers between devices with their start and end apart: 8, of which 3 were waited for; matrix products, arithmetic and copies ran while one was open for 0% of the time, Pallas kernels for 0%

profile of v1, /device:TPU:0, one launch (start us, length us, event | category | flops | bytes accessed | tf_op | source)
XLA Modules:
  0.0 180.0 jit_solution(927660027667059949)
XLA Ops:
  0.0 70.2 %all-gather = s32[32,2,16]{2,1,0:T(2,128)S(1)} all-gather(s32[1,2,16]{2,1,0:T(2,128)} %bitcast.45), channel_id=1, replica_groups=mesh['pb'=4,'dev'=8] {'pb','dev'}, dimensions={0}, use_global_device_ids=true | all-gather | bytes 4224 | tf_op jit(solution)/shard_map/all_gather | solution.py:59
  70.3 0.7 and_reduce_fusion
  71.0 0.7 multiply_reduce_fusion
  71.8 0.1 copy.16
  71.8 0.1 reshape.61
  71.9 7.7 %scatter_custom_fusion = bf16[65536]{0:T(1024)(128)(2,1)S(1)} fusion(s32[1024]{0:T(1024)S(1)} %reshape.61, bf16[1024]{0:T(1024)(128)(2,1)S(1)} %broadcast.93, bf16[]{:T(256)} %constant.54.clone.1), kind=kCustom, calls=%fused_computation.7 | custom fusion | bytes 131074
  79.6 0.1 reshape.52
  79.7 64.1 %all-gather.1 = bf16[32,2,768]{2,1,0:T(2,128)(2,1)S(1)} all-gather(bf16[1,2,768]{2,1,0:T(2,128)(2,1)} %bitcast.44), channel_id=1, replica_groups=mesh['pb'=4,'dev'=8] {'pb','dev'}, dimensions={0}, use_global_device_ids=true | all-gather | bytes 101376 | tf_op jit(solution)/shard_map/all_gather | solution.py:59
  143.8 0.5 fusion.1
  144.3 0.4 convolution_select_fusion
  144.7 3.8 %sort_prefixfusion = f32[64,100]{1,0:T(8,128)} fusion(f32[64,512]{1,0:T(8,128)S(1)} %convolution_select_fusion), kind=kCustom, calls=%top_k.14.sort_prefix | custom fusion | flops 491520 | bytes 156672 | tf_op jit(solution)/shard_map/while/body/eval_jaxpr/top_k | solution.py:65
  148.5 3.4 %all-to-all-start = ((f32[4,16,100]{2,1,0:T(8,128)}), f32[4,16,100]{2,1,0:T(8,128)S(1)}, u32[]{:S(2)}, u32[]{:S(2)}) async-start(f32[4,16,100]{2,1,0:T(8,128)} %bitcast.4), calls=%async_computation | async-start | bytes 65536 | tf_op jit(solution)/shard_map/all_to_all | solution.py:79
  152.0 3.7 %all-to-all-done = f32[4,16,100]{2,1,0:T(8,128)S(1)} async-done(((f32[4,16,100]{2,1,0:T(8,128)}), f32[4,16,100]{2,1,0:T(8,128)S(1)}, u32[]{:S(2)}, u32[]{:S(2)}) %all-to-all-start) | async-done | bytes 25632 | tf_op jit(solution)/shard_map/all_to_all | solution.py:79
  155.7 0.1 reshape.47
  155.8 2.3 %collective-permute-start = (f32[2,400]{1,0:T(2,128)S(1)}, f32[2,400]{1,0:T(2,128)S(1)}, u32[]{:S(2)}, u32[]{:S(2)}) collective-permute-start(f32[2,400]{1,0:T(2,128)S(1)} %get-tuple-element.36), channel_id=1, source_target_pairs={{0,1},{1,0},{2,3},{3,2},{4,5},{5,4},{6,7},{7,6},{8,9},{9,8},{10,11... | collective-permute-start | bytes 9608 | tf_op jit(solution)/shard_map/ppermute | solution.py:34
  158.1 1.5 collective-permute-start.2
  159.7 4.3 %collective-permute-start.4 = (f32[2,400]{1,0:T(2,128)S(1)}, f32[2,400]{1,0:T(2,128)S(1)}, u32[]{:S(2)}, u32[]{:S(2)}) collective-permute-start(f32[2,400]{1,0:T(2,128)S(1)} %get-tuple-element.32), channel_id=1, source_target_pairs={{0,5},{1,4},{2,7},{3,6},{4,1},{5,0},{6,3},{7,2},{8,13},{9,12},{10,... | collective-permute-start | bytes 9608 | tf_op jit(solution)/shard_map/ppermute | solution.py:34
  164.0 3.3 %collective-permute-start.6 = (f32[2,400]{1,0:T(2,128)S(1)}, f32[2,400]{1,0:T(2,128)S(1)}, u32[]{:S(2)}, u32[]{:S(2)}) collective-permute-start(f32[2,400]{1,0:T(2,128)S(1)} %get-tuple-element.30), channel_id=1, source_target_pairs={{0,7},{1,6},{2,5},{3,4},{4,3},{5,2},{6,1},{7,0},{8,15},{9,14},{10,... | collective-permute-start | bytes 9608 | tf_op jit(solution)/shard_map/ppermute | solution.py:34
  167.4 2.0 %collective-permute-done.5 = f32[2,400]{1,0:T(2,128)S(1)} collective-permute-done((f32[2,400]{1,0:T(2,128)S(1)}, f32[2,400]{1,0:T(2,128)S(1)}, u32[]{:S(2)}, u32[]{:S(2)}) %collective-permute-start.5) | collective-permute-done | bytes 3232 | tf_op jit(solution)/shard_map/ppermute | solution.py:34
  169.4 1.0 collective-permute-done.6
  170.4 0.6 gather_fusion
  171.0 0.1 reshape.48
  171.1 8.4 %top_k.20 = (f32[2,3200]{1,0:T(2,128)S(1)}, s32[2,3200]{1,0:T(2,128)}) sort(f32[2,3200]{1,0:T(2,128)S(1)} %reshape.48, s32[2,3200]{1,0:T(2,128)S(1)} %iota.29), dimensions={1}, to_apply=%region_2.3 | sort | flops 83200 | bytes 102400 | tf_op jit(solution)/shard_map/top_k | solution.py:81
  179.5 0.6 top_k.21
  (31 shorter events, 0.3 us)
Async XLA Ops:
  0.0 144.3 %copy-start = (bf16[512,768]{1,0:T(8,128)(2,1)S(1)}, bf16[512,768]{1,0:T(8,128)(2,1)}, u32[]{:S(2)}) copy-start(bf16[512,768]{1,0:T(8,128)(2,1)} %param.6) | copy-start | bytes 2359300
  0.0 143.8 %copy-start.1 = (s32[512]{0:T(512)S(1)}, s32[512]{0:T(512)}, u32[]{:S(2)}) copy-start(s32[512]{0:T(512)} %param.7) | copy-start | bytes 6148
  148.5 7.2 %all-to-all-start = ((f32[4,16,100]{2,1,0:T(8,128)}), f32[4,16,100]{2,1,0:T(8,128)S(1)}, u32[]{:S(2)}, u32[]{:S(2)}) async-start(f32[4,16,100]{2,1,0:T(8,128)} %bitcast.4), calls=%async_computation | async-start | bytes 65536 | tf_op jit(solution)/shard_map/all_to_all | solution.py:79
  155.8 8.1 %collective-permute-start = (f32[2,400]{1,0:T(2,128)S(1)}, f32[2,400]{1,0:T(2,128)S(1)}, u32[]{:S(2)}, u32[]{:S(2)}) collective-permute-start(f32[2,400]{1,0:T(2,128)S(1)} %get-tuple-element.36), channel_id=1, source_target_pairs={{0,1},{1,0},{2,3},{3,2},{4,5},{5,4},{6,7},{7,6},{8,9},{9,8},{10,11... | collective-permute-start | bytes 9608 | tf_op jit(solution)/shard_map/ppermute | solution.py:34
  158.1 5.9 %collective-permute-start.1 = (f32[2,400]{1,0:T(2,128)S(1)}, f32[2,400]{1,0:T(2,128)S(1)}, u32[]{:S(2)}, u32[]{:S(2)}) collective-permute-start(f32[2,400]{1,0:T(2,128)S(1)} %get-tuple-element.35), channel_id=1, source_target_pairs={{0,2},{1,3},{2,0},{3,1},{4,6},{5,7},{6,4},{7,5},{8,10},{9,11},{10,... | collective-permute-start | bytes 9608 | tf_op jit(solution)/shard_map/ppermute | solution.py:34
  158.1 9.2 %collective-permute-start.2 = (f32[2,400]{1,0:T(2,128)S(1)}, f32[2,400]{1,0:T(2,128)S(1)}, u32[]{:S(2)}, u32[]{:S(2)}) collective-permute-start(f32[2,400]{1,0:T(2,128)S(1)} %get-tuple-element.34), channel_id=1, source_target_pairs={{0,3},{1,2},{2,1},{3,0},{4,7},{5,6},{6,5},{7,4},{8,11},{9,10},{10,... | collective-permute-start | bytes 9608 | tf_op jit(solution)/shard_map/ppermute | solution.py:34
  159.7 7.7 %collective-permute-start.3 = (f32[2,400]{1,0:T(2,128)S(1)}, f32[2,400]{1,0:T(2,128)S(1)}, u32[]{:S(2)}, u32[]{:S(2)}) collective-permute-start(f32[2,400]{1,0:T(2,128)S(1)} %get-tuple-element.33), channel_id=1, source_target_pairs={{0,4},{1,5},{2,6},{3,7},{4,0},{5,1},{6,2},{7,3},{8,12},{9,13},{10,... | collective-permute-start | bytes 9608 | tf_op jit(solution)/shard_map/ppermute | solution.py:34
  159.7 7.7 %collective-permute-start.4 = (f32[2,400]{1,0:T(2,128)S(1)}, f32[2,400]{1,0:T(2,128)S(1)}, u32[]{:S(2)}, u32[]{:S(2)}) collective-permute-start(f32[2,400]{1,0:T(2,128)S(1)} %get-tuple-element.32), channel_id=1, source_target_pairs={{0,5},{1,4},{2,7},{3,6},{4,1},{5,0},{6,3},{7,2},{8,13},{9,12},{10,... | collective-permute-start | bytes 9608 | tf_op jit(solution)/shard_map/ppermute | solution.py:34
  164.0 5.4 %collective-permute-start.5 = (f32[2,400]{1,0:T(2,128)S(1)}, f32[2,400]{1,0:T(2,128)S(1)}, u32[]{:S(2)}, u32[]{:S(2)}) collective-permute-start(f32[2,400]{1,0:T(2,128)S(1)} %get-tuple-element.31), channel_id=1, source_target_pairs={{0,6},{1,7},{2,4},{3,5},{4,2},{5,3},{6,0},{7,1},{8,14},{9,15},{10,... | collective-permute-start | bytes 9608 | tf_op jit(solution)/shard_map/ppermute | solution.py:34
  164.0 6.4 %collective-permute-start.6 = (f32[2,400]{1,0:T(2,128)S(1)}, f32[2,400]{1,0:T(2,128)S(1)}, u32[]{:S(2)}, u32[]{:S(2)}) collective-permute-start(f32[2,400]{1,0:T(2,128)S(1)} %get-tuple-element.30), channel_id=1, source_target_pairs={{0,7},{1,6},{2,5},{3,4},{4,3},{5,2},{6,1},{7,0},{8,15},{9,14},{10,... | collective-permute-start | bytes 9608 | tf_op jit(solution)/shard_map/ppermute | solution.py:34
